TPU v7x, 256 devices: a whole 4x4x8 slice. The times are simulated.
256 devices in a mesh: rep: 2 (over x_hi), px: 8 (over y, core), py: 16 (over z, x_lo).
Axes of the slice: x: 4 (x_hi: 2, x_lo: 2; x = x_hi * 2 + x_lo), y: 4, z: 8, core: 2. Of those that a mesh axis runs over, the one named last changes fastest.
Arguments:
- density: float32 [4, 128, 128, 128], P('rep', 'px', 'py'), parts along dimension 0, may hold values from -6 to 6
- kernel_factors: float32 [3, 89, 256], replicated, as said below
Outputs:
- potential: float32 [4, 128, 128, 128], P('rep', 'px', 'py'), parts along dimension 0
There are 2 independent parts, one for each index of `rep`. A program takes and returns all parts, laid end to end along the dimension named above; an argument that names none is the same for every part. Nothing has to cross between parts.
Inputs may be any that keep to these rules, and one draw needn't show every extreme that they name: Each factor is even in its frequency, kernel_factors[d, g, k] = kernel_factors[d, g, 256 - k], and is zero at k = 128.
All inputs are finite; a program needn't handle non-finite values.
Results may differ from a plain program's by a relative error of at most 0.00005.
Values sent between devices are 32-bit elements; how exact they have to be, the bound alone decides.
A program may use at most 64 MiB of HBM per device.

v0:
```python
import math

import jax
import jax.numpy as jnp
from jax import lax
from jax.sharding import PartitionSpec as P


def phases(out_index, in_index, period):
    product = out_index[:, None] * in_index[None, :] % period
    return product.astype(jnp.float32) * (2.0 * math.pi / period)


def along_last(table, values):
    return jnp.einsum(
        "kl,abl->kab",
        table,
        values,
        precision=lax.Precision.HIGHEST,
        preferred_element_type=jnp.float32,
    )


def along_first(values, table):
    return jnp.einsum(
        "kab,kl->abl",
        values,
        table,
        precision=lax.Precision.HIGHEST,
        preferred_element_type=jnp.float32,
    )


def forward_table(length, period, count):
    angles = phases(jnp.arange(count, dtype=jnp.int32), jnp.arange(length, dtype=jnp.int32), period)
    return jnp.concatenate([jnp.cos(angles), jnp.sin(angles)], 0)


def inverse_table(length, period):
    angles = phases(
        jnp.arange(period, dtype=jnp.int32), jnp.arange(length, dtype=jnp.int32), period
    )
    return jnp.concatenate([jnp.cos(angles), jnp.sin(angles)], 1)


def forward_pair(table, real_part, imag_part):
    count = table.shape[0] // 2
    from_real = along_last(table, real_part)
    from_imag = along_last(table, imag_part)
    return (from_real[:count] + from_imag[count:], from_imag[:count] - from_real[count:])


def inverse_pair(table, real_part, imag_part):
    length = table.shape[1] // 2
    from_real = along_first(real_part, table)
    from_imag = along_first(imag_part, table)
    return (
        from_real[..., :length] - from_imag[..., length:],
        from_real[..., length:] + from_imag[..., :length],
    )


def kernel_block(kernel_factors, y_start, y_count, z_start, z_count):
    terms = kernel_factors.shape[1]
    period = kernel_factors.shape[2]
    factor_y = lax.dynamic_slice_in_dim(kernel_factors[1], y_start, y_count, 1)
    factor_z = lax.dynamic_slice_in_dim(kernel_factors[2], z_start, z_count, 1)
    pair_yz = (factor_y[:, :, None] * factor_z[:, None, :]).reshape(terms, y_count * z_count)
    kernel = jnp.einsum("gx,gq->xq", kernel_factors[0], pair_yz, precision=lax.Precision.HIGHEST)
    return kernel.reshape(period, y_count, z_count)


def body(density, kernel_factors):
    replicas = density.shape[0]
    length = density.shape[3]
    period = 2 * length
    count_px = lax.axis_size("px")
    count_py = lax.axis_size("py")
    index_px = lax.axis_index("px")
    index_py = lax.axis_index("py")
    z_weights = jnp.where(jnp.arange(length, dtype=jnp.int32) == 0, 1.0, 2.0).astype(jnp.float32)
    real_table = forward_table(length, period, length)
    complex_table = forward_table(length, period, period)
    back_table = inverse_table(length, period)
    parts = []
    for replica in range(replicas):
        projected = along_last(real_table, density[replica])
        parts.append(projected[:length])
        parts.append(-projected[length:])
    parts = lax.all_to_all(tuple(parts), "py", split_axis=0, concat_axis=2, tiled=True)
    parts = list(parts)
    for replica in range(replicas):
        parts[2 * replica], parts[2 * replica + 1] = forward_pair(
            complex_table, parts[2 * replica], parts[2 * replica + 1]
        )
    parts = list(lax.all_to_all(tuple(parts), "px", split_axis=0, concat_axis=2, tiled=True))
    y_rows = period // count_px
    z_rows = length // count_py
    kernel = kernel_block(kernel_factors, index_px * y_rows, y_rows, index_py * z_rows, z_rows)
    for replica in range(replicas):
        real_part, imag_part = forward_pair(
            complex_table, parts[2 * replica], parts[2 * replica + 1]
        )
        parts[2 * replica], parts[2 * replica + 1] = inverse_pair(
            back_table, real_part * kernel, imag_part * kernel
        )
    parts = list(lax.all_to_all(tuple(parts), "px", split_axis=2, concat_axis=0, tiled=True))
    for replica in range(replicas):
        parts[2 * replica], parts[2 * replica + 1] = inverse_pair(
            back_table, parts[2 * replica], parts[2 * replica + 1]
        )
    parts = list(lax.all_to_all(tuple(parts), "py", split_axis=2, concat_axis=0, tiled=True))
    angles = phases(
        jnp.arange(length, dtype=jnp.int32), jnp.arange(length, dtype=jnp.int32), period
    )
    scaled = (z_weights * (1.0 / float(period) ** 3))[:, None]
    cos_table = jnp.cos(angles) * scaled
    sine_table = -jnp.sin(angles) * scaled
    results = []
    for replica in range(replicas):
        field = along_first(parts[2 * replica], cos_table) + along_first(
            parts[2 * replica + 1], sine_table
        )
        results.append(field)
    return jnp.stack(results, 0)


def solution(mesh):
    placed = (P("rep", "px", "py", None), P())
    return jax.shard_map(
        body, mesh=mesh, in_specs=placed, out_specs=P("rep", "px", "py", None), check_vma=False
    )
```

profile of v0, /device:TPU:4, one launch (start us, length us, event | category | flops | bytes accessed | tf_op | source)
XLA Modules:
  0.0 196.0 jit_solution(18144600202474491138)
XLA Ops:
  2.3 9.2 %all-to-all-start.9 = ((f32[16,1,1024]{2,1,0:T(1,128)}), f32[16,1,1024]{2,1,0:T(1,128)S(1)}, u32[]{:S(2)}, u32[]{:S(2)}) async-start(f32[16,1,1024]{2,1,0:T(1,128)} %reshape.34), calls=%async_computation.9 | async-start | bytes 131072 | tf_op jit(solution)/shard_map/all_to_all | solution.py:90
  14.0 6.6 %all-to-all-done.9 = f32[16,1,1024]{2,1,0:T(1,128)S(1)} async-done(((f32[16,1,1024]{2,1,0:T(1,128)}), f32[16,1,1024]{2,1,0:T(1,128)S(1)}, u32[]{:S(2)}, u32[]{:S(2)}) %all-to-all-start.9) | async-done | bytes 65568 | tf_op jit(solution)/shard_map/all_to_all | solution.py:90
  20.6 3.5 %all-to-all-start.8 = ((f32[16,1,1024]{2,1,0:T(1,128)}), f32[16,1,1024]{2,1,0:T(1,128)S(1)}, u32[]{:S(2)}, u32[]{:S(2)}) async-start(f32[16,1,1024]{2,1,0:T(1,128)} %reshape.36), calls=%async_computation.8 | async-start | bytes 131072 | tf_op jit(solution)/shard_map/all_to_all | solution.py:90
  29.4 3.7 %all-to-all-done.8 = f32[16,1,1024]{2,1,0:T(1,128)S(1)} async-done(((f32[16,1,1024]{2,1,0:T(1,128)}), f32[16,1,1024]{2,1,0:T(1,128)S(1)}, u32[]{:S(2)}, u32[]{:S(2)}) %all-to-all-start.8) | async-done | bytes 65568 | tf_op jit(solution)/shard_map/all_to_all | solution.py:90
  33.1 4.4 %all-to-all-start.1 = ((f32[16,1,1024]{2,1,0:T(1,128)}), f32[16,1,1024]{2,1,0:T(1,128)S(1)}, u32[]{:S(2)}, u32[]{:S(2)}) async-start(f32[16,1,1024]{2,1,0:T(1,128)} %reshape.50), calls=%async_computation.1 | async-start | bytes 131072 | tf_op jit(solution)/shard_map/all_to_all | solution.py:90
  42.1 4.5 %all-to-all-done.1 = f32[16,1,1024]{2,1,0:T(1,128)S(1)} async-done(((f32[16,1,1024]{2,1,0:T(1,128)}), f32[16,1,1024]{2,1,0:T(1,128)S(1)}, u32[]{:S(2)}, u32[]{:S(2)}) %all-to-all-start.1) | async-done | bytes 65568 | tf_op jit(solution)/shard_map/all_to_all | solution.py:90
  46.6 3.7 %all-to-all-start = ((f32[16,1,1024]{2,1,0:T(1,128)}), f32[16,1,1024]{2,1,0:T(1,128)S(1)}, u32[]{:S(2)}, u32[]{:S(2)}) async-start(f32[16,1,1024]{2,1,0:T(1,128)} %reshape.52), calls=%async_computation | async-start | bytes 131072 | tf_op jit(solution)/shard_map/all_to_all | solution.py:90
  52.2 7.0 %all-to-all-done = f32[16,1,1024]{2,1,0:T(1,128)S(1)} async-done(((f32[16,1,1024]{2,1,0:T(1,128)}), f32[16,1,1024]{2,1,0:T(1,128)S(1)}, u32[]{:S(2)}, u32[]{:S(2)}) %all-to-all-start) | async-done | bytes 65568 | tf_op jit(solution)/shard_map/all_to_all | solution.py:90
  59.3 4.5 %all-to-all-start.11 = ((f32[8,1,4096]{2,1,0:T(1,128)}), f32[8,1,4096]{2,1,0:T(1,128)S(1)}, u32[]{:S(2)}, u32[]{:S(2)}) async-start(f32[8,1,4096]{2,1,0:T(1,128)} %reshape.40), calls=%async_computation.11 | async-start | bytes 262144 | tf_op jit(solution)/shard_map/all_to_all | solution.py:96
  70.2 4.8 %all-to-all-start.10 = ((f32[8,1,4096]{2,1,0:T(1,128)}), f32[8,1,4096]{2,1,0:T(1,128)S(1)}, u32[]{:S(2)}, u32[]{:S(2)}) async-start(f32[8,1,4096]{2,1,0:T(1,128)} %reshape.38), calls=%async_computation.10 | async-start | bytes 262144 | tf_op jit(solution)/shard_map/all_to_all | solution.py:96
  76.7 1.1 fusion.89
  77.8 3.3 %all-to-all-done.10 = f32[8,1,4096]{2,1,0:T(1,128)S(1)} async-done(((f32[8,1,4096]{2,1,0:T(1,128)}), f32[8,1,4096]{2,1,0:T(1,128)S(1)}, u32[]{:S(2)}, u32[]{:S(2)}) %all-to-all-start.10) | async-done | bytes 131104 | tf_op jit(solution)/shard_map/all_to_all | solution.py:96
  81.1 3.4 %all-to-all-start.2 = ((f32[8,1,4096]{2,1,0:T(1,128)}), f32[8,1,4096]{2,1,0:T(1,128)S(1)}, u32[]{:S(2)}, u32[]{:S(2)}) async-start(f32[8,1,4096]{2,1,0:T(1,128)} %reshape.54), calls=%async_computation.2 | async-start | bytes 262144 | tf_op jit(solution)/shard_map/all_to_all | solution.py:96
  87.3 3.2 %all-to-all-done.2 = f32[8,1,4096]{2,1,0:T(1,128)S(1)} async-done(((f32[8,1,4096]{2,1,0:T(1,128)}), f32[8,1,4096]{2,1,0:T(1,128)S(1)}, u32[]{:S(2)}, u32[]{:S(2)}) %all-to-all-start.2) | async-done | bytes 131104 | tf_op jit(solution)/shard_map/all_to_all | solution.py:96
  90.5 3.4 %all-to-all-start.3 = ((f32[8,1,4096]{2,1,0:T(1,128)}), f32[8,1,4096]{2,1,0:T(1,128)S(1)}, u32[]{:S(2)}, u32[]{:S(2)}) async-start(f32[8,1,4096]{2,1,0:T(1,128)} %reshape.56), calls=%async_computation.3 | async-start | bytes 262144 | tf_op jit(solution)/shard_map/all_to_all | solution.py:96
  96.7 3.2 %all-to-all-done.3 = f32[8,1,4096]{2,1,0:T(1,128)S(1)} async-done(((f32[8,1,4096]{2,1,0:T(1,128)}), f32[8,1,4096]{2,1,0:T(1,128)S(1)}, u32[]{:S(2)}, u32[]{:S(2)}) %all-to-all-start.3) | async-done | bytes 131104 | tf_op jit(solution)/shard_map/all_to_all | solution.py:96
  105.2 3.4 %all-to-all-start.4 = ((f32[8,1,4096]{2,1,0:T(1,128)}), f32[8,1,4096]{2,1,0:T(1,128)S(1)}, u32[]{:S(2)}, u32[]{:S(2)}) async-start(f32[8,1,4096]{2,1,0:T(1,128)} %reshape.60), calls=%async_computation.4 | async-start | bytes 262144 | tf_op jit(solution)/shard_map/all_to_all | solution.py:107
  113.1 1.5 all-to-all-done.4
  114.6 3.6 %all-to-all-start.5 = ((f32[8,1,4096]{2,1,0:T(1,128)}), f32[8,1,4096]{2,1,0:T(1,128)S(1)}, u32[]{:S(2)}, u32[]{:S(2)}) async-start(f32[8,1,4096]{2,1,0:T(1,128)} %reshape.58), calls=%async_computation.5 | async-start | bytes 262144 | tf_op jit(solution)/shard_map/all_to_all | solution.py:107
  120.1 3.9 %all-to-all-done.5 = f32[8,1,4096]{2,1,0:T(1,128)S(1)} async-done(((f32[8,1,4096]{2,1,0:T(1,128)}), f32[8,1,4096]{2,1,0:T(1,128)S(1)}, u32[]{:S(2)}, u32[]{:S(2)}) %all-to-all-start.5) | async-done | bytes 131104 | tf_op jit(solution)/shard_map/all_to_all | solution.py:107
  124.0 3.4 %all-to-all-start.12 = ((f32[8,1,4096]{2,1,0:T(1,128)}), f32[8,1,4096]{2,1,0:T(1,128)S(1)}, u32[]{:S(2)}, u32[]{:S(2)}) async-start(f32[8,1,4096]{2,1,0:T(1,128)} %reshape.44), calls=%async_computation.12 | async-start | bytes 262144 | tf_op jit(solution)/shard_map/all_to_all | solution.py:107
  129.3 4.1 %all-to-all-done.12 = f32[8,1,4096]{2,1,0:T(1,128)S(1)} async-done(((f32[8,1,4096]{2,1,0:T(1,128)}), f32[8,1,4096]{2,1,0:T(1,128)S(1)}, u32[]{:S(2)}, u32[]{:S(2)}) %all-to-all-start.12) | async-done | bytes 131104 | tf_op jit(solution)/shard_map/all_to_all | solution.py:107
  133.4 3.4 %all-to-all-start.13 = ((f32[8,1,4096]{2,1,0:T(1,128)}), f32[8,1,4096]{2,1,0:T(1,128)S(1)}, u32[]{:S(2)}, u32[]{:S(2)}) async-start(f32[8,1,4096]{2,1,0:T(1,128)} %reshape.42), calls=%async_computation.13 | async-start | bytes 262144 | tf_op jit(solution)/shard_map/all_to_all | solution.py:107
  140.9 1.9 all-to-all-done.13
  142.8 3.5 %all-to-all-start.6 = ((f32[16,1,1024]{2,1,0:T(1,128)}), f32[16,1,1024]{2,1,0:T(1,128)S(1)}, u32[]{:S(2)}, u32[]{:S(2)}) async-start(f32[16,1,1024]{2,1,0:T(1,128)} %reshape.62), calls=%async_computation.6 | async-start | bytes 131072 | tf_op jit(solution)/shard_map/all_to_all | solution.py:112
  148.2 7.2 %all-to-all-done.6 = f32[16,1,1024]{2,1,0:T(1,128)S(1)} async-done(((f32[16,1,1024]{2,1,0:T(1,128)}), f32[16,1,1024]{2,1,0:T(1,128)S(1)}, u32[]{:S(2)}, u32[]{:S(2)}) %all-to-all-start.6) | async-done | bytes 65568 | tf_op jit(solution)/shard_map/all_to_all | solution.py:112
  155.3 3.5 %all-to-all-start.7 = ((f32[16,1,1024]{2,1,0:T(1,128)}), f32[16,1,1024]{2,1,0:T(1,128)S(1)}, u32[]{:S(2)}, u32[]{:S(2)}) async-start(f32[16,1,1024]{2,1,0:T(1,128)} %reshape.64), calls=%async_computation.7 | async-start | bytes 131072 | tf_op jit(solution)/shard_map/all_to_all | solution.py:112
  160.0 7.9 %all-to-all-done.7 = f32[16,1,1024]{2,1,0:T(1,128)S(1)} async-done(((f32[16,1,1024]{2,1,0:T(1,128)}), f32[16,1,1024]{2,1,0:T(1,128)S(1)}, u32[]{:S(2)}, u32[]{:S(2)}) %all-to-all-start.7) | async-done | bytes 65568 | tf_op jit(solution)/shard_map/all_to_all | solution.py:112
  167.9 3.5 %all-to-all-start.14 = ((f32[16,1,1024]{2,1,0:T(1,128)}), f32[16,1,1024]{2,1,0:T(1,128)S(1)}, u32[]{:S(2)}, u32[]{:S(2)}) async-start(f32[16,1,1024]{2,1,0:T(1,128)} %reshape.46), calls=%async_computation.14 | async-start | bytes 131072 | tf_op jit(solution)/shard_map/all_to_all | solution.py:112
  175.1 5.4 %all-to-all-done.14 = f32[16,1,1024]{2,1,0:T(1,128)S(1)} async-done(((f32[16,1,1024]{2,1,0:T(1,128)}), f32[16,1,1024]{2,1,0:T(1,128)S(1)}, u32[]{:S(2)}, u32[]{:S(2)}) %all-to-all-start.14) | async-done | bytes 65568 | tf_op jit(solution)/shard_map/all_to_all | solution.py:112
  180.5 3.5 %all-to-all-start.15 = ((f32[16,1,1024]{2,1,0:T(1,128)}), f32[16,1,1024]{2,1,0:T(1,128)S(1)}, u32[]{:S(2)}, u32[]{:S(2)}) async-start(f32[16,1,1024]{2,1,0:T(1,128)} %reshape.48), calls=%async_computation.15 | async-start | bytes 131072 | tf_op jit(solution)/shard_map/all_to_all | solution.py:112
  186.2 6.8 %all-to-all-done.15 = f32[16,1,1024]{2,1,0:T(1,128)S(1)} async-done(((f32[16,1,1024]{2,1,0:T(1,128)}), f32[16,1,1024]{2,1,0:T(1,128)S(1)}, u32[]{:S(2)}, u32[]{:S(2)}) %all-to-all-start.15) | async-done | bytes 65568 | tf_op jit(solution)/shard_map/all_to_all | solution.py:112
  (133 shorter events, 59.3 us)
Async XLA Ops:
  0.0 0.9 copy-start.2
  2.3 18.3 %all-to-all-start.9 = ((f32[16,1,1024]{2,1,0:T(1,128)}), f32[16,1,1024]{2,1,0:T(1,128)S(1)}, u32[]{:S(2)}, u32[]{:S(2)}) async-start(f32[16,1,1024]{2,1,0:T(1,128)} %reshape.34), calls=%async_computation.9 | async-start | bytes 131072 | tf_op jit(solution)/shard_map/all_to_all | solution.py:90
  12.6 1.0 copy-start.1
  20.6 12.6 %all-to-all-start.8 = ((f32[16,1,1024]{2,1,0:T(1,128)}), f32[16,1,1024]{2,1,0:T(1,128)S(1)}, u32[]{:S(2)}, u32[]{:S(2)}) async-start(f32[16,1,1024]{2,1,0:T(1,128)} %reshape.36), calls=%async_computation.8 | async-start | bytes 131072 | tf_op jit(solution)/shard_map/all_to_all | solution.py:90
  33.1 13.4 %all-to-all-start.1 = ((f32[16,1,1024]{2,1,0:T(1,128)}), f32[16,1,1024]{2,1,0:T(1,128)S(1)}, u32[]{:S(2)}, u32[]{:S(2)}) async-start(f32[16,1,1024]{2,1,0:T(1,128)} %reshape.50), calls=%async_computation.1 | async-start | bytes 131072 | tf_op jit(solution)/shard_map/all_to_all | solution.py:90
  46.6 12.7 %all-to-all-start = ((f32[16,1,1024]{2,1,0:T(1,128)}), f32[16,1,1024]{2,1,0:T(1,128)S(1)}, u32[]{:S(2)}, u32[]{:S(2)}) async-start(f32[16,1,1024]{2,1,0:T(1,128)} %reshape.52), calls=%async_computation | async-start | bytes 131072 | tf_op jit(solution)/shard_map/all_to_all | solution.py:90
  59.3 10.9 %all-to-all-start.11 = ((f32[8,1,4096]{2,1,0:T(1,128)}), f32[8,1,4096]{2,1,0:T(1,128)S(1)}, u32[]{:S(2)}, u32[]{:S(2)}) async-start(f32[8,1,4096]{2,1,0:T(1,128)} %reshape.40), calls=%async_computation.11 | async-start | bytes 262144 | tf_op jit(solution)/shard_map/all_to_all | solution.py:96
  70.2 10.9 %all-to-all-start.10 = ((f32[8,1,4096]{2,1,0:T(1,128)}), f32[8,1,4096]{2,1,0:T(1,128)S(1)}, u32[]{:S(2)}, u32[]{:S(2)}) async-start(f32[8,1,4096]{2,1,0:T(1,128)} %reshape.38), calls=%async_computation.10 | async-start | bytes 262144 | tf_op jit(solution)/shard_map/all_to_all | solution.py:96
  81.1 9.4 %all-to-all-start.2 = ((f32[8,1,4096]{2,1,0:T(1,128)}), f32[8,1,4096]{2,1,0:T(1,128)S(1)}, u32[]{:S(2)}, u32[]{:S(2)}) async-start(f32[8,1,4096]{2,1,0:T(1,128)} %reshape.54), calls=%async_computation.2 | async-start | bytes 262144 | tf_op jit(solution)/shard_map/all_to_all | solution.py:96
  90.5 9.4 %all-to-all-start.3 = ((f32[8,1,4096]{2,1,0:T(1,128)}), f32[8,1,4096]{2,1,0:T(1,128)S(1)}, u32[]{:S(2)}, u32[]{:S(2)}) async-start(f32[8,1,4096]{2,1,0:T(1,128)} %reshape.56), calls=%async_computation.3 | async-start | bytes 262144 | tf_op jit(solution)/shard_map/all_to_all | solution.py:96
  101.6 1.1 copy-start
  105.2 9.4 %all-to-all-start.4 = ((f32[8,1,4096]{2,1,0:T(1,128)}), f32[8,1,4096]{2,1,0:T(1,128)S(1)}, u32[]{:S(2)}, u32[]{:S(2)}) async-start(f32[8,1,4096]{2,1,0:T(1,128)} %reshape.60), calls=%async_computation.4 | async-start | bytes 262144 | tf_op jit(solution)/shard_map/all_to_all | solution.py:107
  114.6 9.4 %all-to-all-start.5 = ((f32[8,1,4096]{2,1,0:T(1,128)}), f32[8,1,4096]{2,1,0:T(1,128)S(1)}, u32[]{:S(2)}, u32[]{:S(2)}) async-start(f32[8,1,4096]{2,1,0:T(1,128)} %reshape.58), calls=%async_computation.5 | async-start | bytes 262144 | tf_op jit(solution)/shard_map/all_to_all | solution.py:107
  124.0 9.4 %all-to-all-start.12 = ((f32[8,1,4096]{2,1,0:T(1,128)}), f32[8,1,4096]{2,1,0:T(1,128)S(1)}, u32[]{:S(2)}, u32[]{:S(2)}) async-start(f32[8,1,4096]{2,1,0:T(1,128)} %reshape.44), calls=%async_computation.12 | async-start | bytes 262144 | tf_op jit(solution)/shard_map/all_to_all | solution.py:107
  133.4 9.4 %all-to-all-start.13 = ((f32[8,1,4096]{2,1,0:T(1,128)}), f32[8,1,4096]{2,1,0:T(1,128)S(1)}, u32[]{:S(2)}, u32[]{:S(2)}) async-start(f32[8,1,4096]{2,1,0:T(1,128)} %reshape.42), calls=%async_computation.13 | async-start | bytes 262144 | tf_op jit(solution)/shard_map/all_to_all | solution.py:107
  142.8 12.6 %all-to-all-start.6 = ((f32[16,1,1024]{2,1,0:T(1,128)}), f32[16,1,1024]{2,1,0:T(1,128)S(1)}, u32[]{:S(2)}, u32[]{:S(2)}) async-start(f32[16,1,1024]{2,1,0:T(1,128)} %reshape.62), calls=%async_computation.6 | async-start | bytes 131072 | tf_op jit(solution)/shard_map/all_to_all | solution.py:112
  155.3 12.6 %all-to-all-start.7 = ((f32[16,1,1024]{2,1,0:T(1,128)}), f32[16,1,1024]{2,1,0:T(1,128)S(1)}, u32[]{:S(2)}, u32[]{:S(2)}) async-start(f32[16,1,1024]{2,1,0:T(1,128)} %reshape.64), calls=%async_computation.7 | async-start | bytes 131072 | tf_op jit(solution)/shard_map/all_to_all | solution.py:112
  167.9 12.6 %all-to-all-start.14 = ((f32[16,1,1024]{2,1,0:T(1,128)}), f32[16,1,1024]{2,1,0:T(1,128)S(1)}, u32[]{:S(2)}, u32[]{:S(2)}) async-start(f32[16,1,1024]{2,1,0:T(1,128)} %reshape.46), calls=%async_computation.14 | async-start | bytes 131072 | tf_op jit(solution)/shard_map/all_to_all | solution.py:112
  180.5 12.6 %all-to-all-start.15 = ((f32[16,1,1024]{2,1,0:T(1,128)}), f32[16,1,1024]{2,1,0:T(1,128)S(1)}, u32[]{:S(2)}, u32[]{:S(2)}) async-start(f32[16,1,1024]{2,1,0:T(1,128)} %reshape.48), calls=%async_computation.15 | async-start | bytes 131072 | tf_op jit(solution)/shard_map/all_to_all | solution.py:112
where the time goes:
time: 198 us; the launch traced here: 196 us
  waiting for transfers between devices  70.3 us (36%)
  starting transfers between devices  64.4 us (33%)
  local copies, waits for them, and re-layouts  29.7 us (15%)
  other arithmetic  15.5 us (8%)
  matrix products  15.2 us (8%)
    all_to_all x4, waiting for transfers between devices, body(): lax.all_to_all(tuple(parts), 'py', split_axis=2, concat_axis=0, tiled=True)  27.3 us
    all_to_all x4, waiting for transfers between devices, body(): lax.all_to_all(tuple(parts), 'py', split_axis=0, concat_axis=2, tiled=True)  21.8 us
    all_to_all x4, starting transfers between devices, body(): lax.all_to_all(tuple(parts), 'py', split_axis=0, concat_axis=2, tiled=True)  20.7 us
    unnamed x40, local copies, waits for them, and re-layouts  19.8 us
    all_to_all x4, starting transfers between devices, body(): lax.all_to_all(tuple(parts), 'px', split_axis=0, concat_axis=2, tiled=True)  16 us
    all_to_all x4, starting transfers between devices, body(): lax.all_to_all(tuple(parts), 'py', split_axis=2, concat_axis=0, tiled=True)  14 us
    all_to_all x4, starting transfers between devices, body(): lax.all_to_all(tuple(parts), 'px', split_axis=2, concat_axis=0, tiled=True)  13.7 us
    all_to_all x4, waiting for transfers between devices, body(): lax.all_to_all(tuple(parts), 'px', split_axis=2, concat_axis=0, tiled=True)  11.5 us
  transfers between devices with their start and end apart: 16, of which 15 were waited for; matrix products, arithmetic and copies ran while one was open for 25% of the time, Pallas kernels for 0%

commit v1 on v0

v1 whole, which is shorter than its diff:
```python
import functools

import jax
import jax.numpy as jnp
import numpy as np
from jax import lax
from jax.experimental import pallas as pl
from jax.experimental.pallas import tpu as pltpu
from jax.sharding import PartitionSpec as P

MESH = pl.DeviceIdType.MESH
N = 128
CHIPS = 64
ROWS_Y = 4
F32, BF16 = jnp.float32, jnp.bfloat16
ORDER = [int(v) + 1 for v in np.random.RandomState(1).permutation(CHIPS - 1)]


def pieces(table):
    table = np.asarray(table, np.float64).astype(np.float32)
    high = table.astype(BF16)
    low = (table - high.astype(np.float32)).astype(BF16)
    return high, low


def tables():
    k, n = np.arange(N), np.arange(N)
    angle = (k[:, None] * n[None, :] % (2 * N)) * (np.pi / N)
    cos, sin = np.cos(angle), np.sin(angle)
    weight = np.where(k == 0, 1.0, 2.0)[:, None] / (2 * N)
    by_owner = np.stack([cos, sin], 1).reshape(2, 2 * CHIPS, N)
    by_owner_back = np.stack([cos * weight, sin * weight], 1).reshape(2, 2 * CHIPS, N)
    plain = np.concatenate([cos, sin], 0)
    back = np.concatenate([cos * weight, sin * weight], 0)
    cells = np.arange(N).reshape(8, 16).T.reshape(-1)
    out = []
    high, low = pieces(by_owner)
    out.append(np.concatenate([high, high, low], 2))
    high, low = pieces(plain.T)
    out.append(np.concatenate([high, high, low], 0))
    high, low = pieces(plain[:, cells])
    out.append(np.concatenate([high, high, low], 1))
    high, low = pieces(back[:, cells].T)
    out.append(np.concatenate([high, low], 0))
    high, low = pieces(back)
    out.append(np.concatenate([high, low], 1))
    high, low = pieces(by_owner_back)
    out.append(np.concatenate([high, low], 2))
    return out


def split(value):
    high = value.astype(BF16)
    return high, (value - high.astype(F32)).astype(BF16)


def dot(a, b, dims=((1,), (0,))):
    return lax.dot_general(a, b, (dims, ((), ())), preferred_element_type=F32)


def swap(blocks):
    group = lax.broadcasted_iota(jnp.int32, (8, N), 1) // 8
    for bit in range(4):
        step = 1 << bit
        low = (group // step) % 2 == 0
        made = list(blocks)
        for i in range(16):
            if i & step:
                continue
            first, second = blocks[i], blocks[i + step]
            made[i] = jnp.where(low, first, pltpu.roll(second, 8 * step, 1))
            made[i + step] = jnp.where(low, pltpu.roll(first, N - 8 * step, 1), second)
        blocks = made
    return blocks


def kernel(
    density, factors, t_z, t_y, t_x, t_xb, t_yb, t_zb, out,
    d_ref, f_ref, z_ref, y_ref, x_ref, xb_ref, yb_ref, zb_ref,
    sa, sb, rf, sr, rb, pb, rows_ref, wide_ref, kernel_ref,
    load, send, recv,
):
    px, py = lax.axis_index("px"), lax.axis_index("py")
    core, y_chip = lax.rem(px, 2), lax.div(px, 2)
    other = 1 - core
    chip = py * ROWS_Y + y_chip
    partner = {"px": px + 1 - 2 * core}

    def peer(offset):
        to = lax.rem(chip + offset, CHIPS)
        return to, {"px": lax.rem(to, ROWS_Y) * 2 + core, "py": lax.div(to, ROWS_Y)}

    barrier = pltpu.get_barrier_semaphore()
    pl.semaphore_signal(barrier, inc=1, device_id=partner, device_id_type=MESH)
    for offset in ORDER:
        pl.semaphore_signal(barrier, inc=1, device_id=peer(offset)[1], device_id_type=MESH)

    loads = [
        pltpu.make_async_copy(src, dst, load.at[i])
        for i, (src, dst) in enumerate(
            [
                (density, d_ref), (t_z, z_ref), (factors.at[:, :, pl.ds(0, N)], f_ref), (t_y, y_ref),
                (t_x, x_ref), (t_xb, xb_ref), (t_yb, yb_ref), (t_zb, zb_ref),
            ]
        )
    ]
    for copy in loads:
        copy.start()
    loads[0].wait()
    loads[1].wait()
    for r in range(2):
        high, low = split(d_ref[r].reshape(N, N))
        both = jnp.concatenate([high, low], 1)
        for owner, to in ((core, sb.at[core, r]), (other, sa.at[r])):
            part = dot(z_ref[owner, :, : 2 * N], both, ((1,), (1,)))
            part += dot(z_ref[owner, :, 2 * N :], high, ((1,), (1,)))
            to[...] = part
    loads[2].wait()
    frequency = core * CHIPS + chip
    lane = lax.broadcasted_iota(jnp.int32, f_ref.shape[1:], 1)
    scale = jnp.sum(jnp.where(lane == frequency, f_ref[2], 0.0), axis=1, keepdims=True)
    kernel_ref[...] = lax.dot_general(
        f_ref[0] * scale, f_ref[1], (((0,), (0,)), ((), ())),
        precision=lax.Precision.HIGHEST, preferred_element_type=F32,
    )
    for copy in loads[3:]:
        copy.wait()

    pl.semaphore_wait(barrier, CHIPS)

    def pair(src, dst, i):
        return pltpu.make_async_remote_copy(
            src_ref=src, dst_ref=dst, send_sem=send.at[i], recv_sem=recv.at[i],
            device_id=partner, device_id_type=MESH,
        )

    def scatter(src, dst, i):
        pltpu.make_async_copy(src(chip), dst, recv.at[i]).start()
        for offset in ORDER:
            to, device = peer(offset)
            pltpu.make_async_remote_copy(
                src_ref=src(to), dst_ref=dst, send_sem=send.at[i], recv_sem=recv.at[i],
                device_id=device, device_id_type=MESH,
            ).start()

    def arrived(whole, i):
        pltpu.make_async_copy(whole, whole, recv.at[i]).wait()

    firsts = [pair(sa.at[r], sb.at[core, r], r) for r in range(2)]
    for copy in firsts:
        copy.start()
    sb5 = sb.reshape(2, 2, CHIPS, 2, N)
    rf5 = rf.reshape(2, CHIPS, 2, 2, N)
    sr5 = sr.reshape(2, CHIPS, 2, 2, N)
    rb5 = rb.reshape(2, 2, CHIPS, 2, N)
    for r in range(2):
        firsts[r].wait_recv()
        scatter(lambda to: sb5.at[:, r, to], rf5.at[r, chip], 2 + r)

    plane = kernel_ref[...]
    wide_plane = jnp.concatenate([plane, plane], 1)
    for r in range(2):
        arrived(rf.at[r], 2 + r)
        for h in range(2):
            blocks = swap([rf[r, pl.ds(16 * i + 8 * h, 8), :] for i in range(16)])
            for i in range(16):
                rows_ref[pl.ds(16 * i + 8 * h, 8), :] = blocks[i]
        high, low = split(rows_ref[...])
        wide = dot(jnp.concatenate([high, low], 1), y_ref[: 2 * N, :]) + dot(high, y_ref[2 * N :, :])
        for half in range(2):
            wide_ref[half] = wide[:, half * N : (half + 1) * N]
        for part in range(2):
            wide = [wide_ref[half, pl.ds(part, N, stride=2), :] for half in range(2)]
            high, low = split(jnp.concatenate(wide, 1))
            both = jnp.concatenate([high, low], 0)
            halves = []
            for half in range(2):
                rows = slice(half * N, (half + 1) * N)
                freq = dot(x_ref[rows, : 2 * N], both) + dot(x_ref[rows, 2 * N :], high)
                halves.append(split(freq * wide_plane))
            high = jnp.concatenate([halves[0][0], halves[1][0]], 0)
            low = jnp.concatenate([halves[0][1], halves[1][1]], 0)
            mixed = dot(xb_ref[:N, :], high) + dot(xb_ref[:N, :], low) + dot(xb_ref[N:, :], high)
            high, low = split(mixed)
            twice = dot(high, yb_ref[...])
            rows_ref[pl.ds(part, N, stride=2), :] = twice[:, :N] + twice[:, N:] + dot(low, yb_ref[:, :N])
        for h in range(2):
            blocks = swap([rows_ref[pl.ds(16 * i + 8 * h, 8), :] for i in range(16)])
            for i in range(16):
                sr[r, pl.ds(16 * i + 8 * h, 8), :] = blocks[i]
        scatter(lambda to: sr5.at[r, to], rb5.at[:, r, chip], 4 + r)

    lasts = [pair(rb.at[other, r], pb.at[r], 6 + r) for r in range(2)]
    for r in range(2):
        arrived(rb.at[:, r], 4 + r)
        lasts[r].start()
        high, low = split(rb[core, r])
        twice = dot(high, zb_ref[core], ((0,), (0,)))
        field = twice[:, :N] + twice[:, N:] + dot(low, zb_ref[core, :, :N], ((0,), (0,)))
        lasts[r].wait_recv()
        high, low = split(pb[r])
        twice = dot(high, zb_ref[other], ((0,), (0,)))
        field += twice[:, :N] + twice[:, N:] + dot(low, zb_ref[other, :, :N], ((0,), (0,)))
        out[r] = field.reshape(16, 8, N)
    for copy in firsts + lasts:
        copy.wait_send()
    for i in range(2, 6):
        some = rf5.at[0, pl.ds(0, CHIPS - 1)]
        pltpu.make_async_copy(some, some, send.at[i]).wait()


def body(density, kernel_factors):
    made = tables()
    held = [pltpu.VMEM(density.shape, F32), pltpu.VMEM(kernel_factors.shape[:2] + (N,), F32)]
    held += [pltpu.VMEM(table.shape, BF16) for table in made]
    scratch = [
        pltpu.VMEM((2, N, N), F32),
        pltpu.VMEM((2, 2, N, N), F32),
        pltpu.VMEM((2, 2 * N, N), F32),
        pltpu.VMEM((2, 2 * N, N), F32),
        pltpu.VMEM((2, 2, N, N), F32),
        pltpu.VMEM((2, N, N), F32),
        pltpu.VMEM((2 * N, N), F32),
        pltpu.VMEM((2, 2 * N, N), F32),
        pltpu.VMEM((N, N), F32),
        pltpu.SemaphoreType.DMA((8,)),
        pltpu.SemaphoreType.DMA((8,)),
        pltpu.SemaphoreType.DMA((8,)),
    ]
    return pl.pallas_call(
        kernel,
        out_shape=jax.ShapeDtypeStruct(density.shape, F32),
        in_specs=[pl.BlockSpec(memory_space=pl.ANY)] * (2 + len(made)),
        out_specs=pl.BlockSpec(memory_space=pltpu.VMEM),
        scratch_shapes=held + scratch,
        compiler_params=pltpu.CompilerParams(collective_id=0, has_side_effects=True),
        name="solve",
    )(density, kernel_factors, *[jnp.asarray(table) for table in made])


def solution(mesh):
    return jax.shard_map(
        body,
        mesh=mesh,
        in_specs=(P("rep", "px", "py", None), P()),
        out_specs=P("rep", "px", "py", None),
        check_vma=False,
    )
```

time: 198 us -> 38.1 us (0.19)
  the two profiles are of different devices: /device:TPU:4 before, /device:TPU:1 now
where the time goes in v1:
time: 38.1 us; the launch traced here: 38 us
  Pallas kernels  36.4 us (96%)
  local copies, waits for them, and re-layouts  1.57 us (4%)
    pallas_call x1, Pallas kernels, body(): pl.pallas_call(kernel, out_shape=jax.ShapeDtypeStruct(density.shape, F32)...  36.4 us
    unnamed x1, local copies, waits for them, and re-layouts  1.57 us

profile of v1, /device:TPU:1, one launch (start us, length us, event | category | flops | bytes accessed | tf_op | source)
XLA Modules:
  0.0 38.0 jit_solution(5624799909627989494)
XLA Ops:
  0.0 36.4 %solve.1 = f32[2,16,8,128]{3,2,1,0:T(8,128)} custom-call(f32[2,16,8,128]{3,2,1,0:T(8,128)} %density.1, f32[3,89,256]{2,1,0:T(8,128)} %factors.1, bf16[2,128,384]{2,1,0:T(8,128)(2,1)} %constant.12.clone.t_z, bf16[384,256]{1,0:T(8,128)(2,1)} %constant.13.clone.t_y, bf16[256,384]{1,0:T(8,128)(2,1)} %constant.14.clone.t_x, ...), custom_call_target="tpu_custom_call" | custom-call | tf_op jit(solution)/shard_map/solve/pallas_call | solution.py:230
  36.4 1.6 %copy.10 = f32[2,16,8,128]{3,2,1,0:T(8,128)} copy(f32[2,16,8,128]{3,2,1,0:T(8,128)} %solve.1) | data formatting | bytes 262144

commit v2 on v1

v2 whole, which is shorter than its diff:
```python
import functools

import jax
import jax.numpy as jnp
import numpy as np
from jax import lax
from jax.experimental import pallas as pl
from jax.experimental.pallas import tpu as pltpu
from jax.sharding import PartitionSpec as P

MESH = pl.DeviceIdType.MESH
N = 128
CHIPS = 64
ROWS_Y = 4
F32, BF16 = jnp.float32, jnp.bfloat16
PARTS = 4
FIRST = 0


def order():
    steps = [(y, z, x) for y in (0, 1, 3, 2) for x in (0, 1) for z in (0, 1, 7, 2, 6, 3, 5, 4) if y or x or z]
    steps = [steps[i] for i in np.random.RandomState(0).permutation(len(steps))]
    return sorted(steps, key=lambda s: -(min(s[0], 4 - s[0]) + min(s[1], 8 - s[1]) + s[2]))


ORDER = order()


def pieces(table):
    table = np.asarray(table, np.float64).astype(np.float32)
    high = table.astype(BF16)
    low = (table - high.astype(np.float32)).astype(BF16)
    return high, low


def tables():
    k, n = np.arange(N), np.arange(N)
    angle = (k[:, None] * n[None, :] % (2 * N)) * (np.pi / N)
    cos, sin = np.cos(angle), np.sin(angle)
    weight = np.where(k == 0, 1.0, 2.0)[:, None] / (2 * N)
    by_owner = np.stack([cos, sin], 0).reshape(2, 2, CHIPS, N).swapaxes(0, 1).reshape(2, 2 * CHIPS, N)
    by_owner_back = np.stack([cos * weight, sin * weight], 0).reshape(2, 2, CHIPS, N).swapaxes(0, 1).reshape(2, 2 * CHIPS, N)
    plain = np.concatenate([cos, sin], 0)
    back = np.concatenate([cos * weight, sin * weight], 0)
    cells = np.arange(N).reshape(8, 16).T.reshape(-1)
    out = []
    high, low = pieces(by_owner)
    out.append(np.concatenate([high, high, low], 2))
    high, low = pieces(plain.T)
    out.append(np.concatenate([high, high, low], 0))
    high, low = pieces(plain[:, cells])
    out.append(np.concatenate([high, high, low], 1))
    high, low = pieces(back[:, cells].T)
    out.append(np.concatenate([high, low], 0))
    high, low = pieces(back)
    out.append(np.concatenate([high, low], 1))
    high, low = pieces(by_owner_back)
    out.append(np.concatenate([high, low], 2))
    return out


def split(value):
    high = value.astype(BF16)
    return high, (value - high.astype(F32)).astype(BF16)


def dot(a, b, dims=((1,), (0,))):
    return lax.dot_general(a, b, (dims, ((), ())), preferred_element_type=F32)


def swap(blocks):
    group = lax.broadcasted_iota(jnp.int32, (8, N), 1) // 8
    for bit in range(4):
        step = 1 << bit
        low = (group // step) % 2 == 0
        made = list(blocks)
        for i in range(16):
            if i & step:
                continue
            first, second = blocks[i], blocks[i + step]
            made[i] = jnp.where(low, first, pltpu.roll(second, 8 * step, 1))
            made[i + step] = jnp.where(low, pltpu.roll(first, N - 8 * step, 1), second)
        blocks = made
    return blocks


def kernel(
    density, factors, t_z, t_y, t_x, t_xb, t_yb, t_zb, out,
    d_ref, f_ref, z_ref, y_ref, x_ref, xb_ref, yb_ref, zb_ref,
    sa, sb, rf, sr, rb, pb, kernel_ref,
    load, send, recv,
):
    px, py = lax.axis_index("px"), lax.axis_index("py")
    core, y_chip = lax.rem(px, 2), lax.div(px, 2)
    x_chip, z_chip = lax.rem(py, 2), lax.div(py, 2)
    other = 1 - core
    chip = py * ROWS_Y + y_chip
    partner = {"px": px + 1 - 2 * core}
    ys = [lax.rem(y_chip + i, 4) for i in range(4)]
    zs = [lax.rem(z_chip + i, 8) for i in range(8)]
    xs = [x_chip, 1 - x_chip]
    peers = []
    for y, z, x in ORDER:
        to = zs[z] * 2 + xs[x]
        peers.append((to * ROWS_Y + ys[y], {"px": ys[y] * 2 + core, "py": to}))

    barrier = pltpu.get_barrier_semaphore()
    for _, device in peers:
        pl.semaphore_signal(barrier, inc=1, device_id=device, device_id_type=MESH)
    pl.semaphore_signal(barrier, inc=1, device_id=partner, device_id_type=MESH)

    loads = [
        pltpu.make_async_copy(src, dst, load.at[i])
        for i, (src, dst) in enumerate(
            [
                (density, d_ref), (t_z, z_ref), (factors.at[:, :, pl.ds(0, N)], f_ref), (t_y, y_ref),
                (t_x, x_ref), (t_xb, xb_ref), (t_yb, yb_ref), (t_zb, zb_ref),
            ]
        )
    ]
    for copy in loads:
        copy.start()
    loads[0].wait()
    loads[1].wait()
    for r in range(2):
        high, low = split(d_ref[r].reshape(N, N))
        both = jnp.concatenate([high, low], 1)
        for owner, mine in ((core, True), (other, False)):
            part = dot(z_ref[owner, :, : 2 * N], both, ((1,), (1,)))
            part += dot(z_ref[owner, :, 2 * N :], high, ((1,), (1,)))
            for i in range(2):
                rows = part[i * CHIPS : (i + 1) * CHIPS]
                if mine:
                    sb[2 * r + i, core] = rows
                else:
                    sa[2 * r + i] = rows
    loads[2].wait()
    frequency = core * CHIPS + chip
    lane = lax.broadcasted_iota(jnp.int32, f_ref.shape[1:], 1)
    scale = jnp.sum(jnp.where(lane == frequency, f_ref[2], 0.0), axis=1, keepdims=True)
    kernel_ref[...] = lax.dot_general(
        f_ref[0] * scale, f_ref[1], (((0,), (0,)), ((), ())),
        precision=lax.Precision.HIGHEST, preferred_element_type=F32,
    )
    for copy in loads[3:]:
        copy.wait()

    pl.semaphore_wait(barrier, CHIPS)

    def pair(src, dst, i):
        return pltpu.make_async_remote_copy(
            src_ref=src, dst_ref=dst, send_sem=send.at[i], recv_sem=recv.at[i],
            device_id=partner, device_id_type=MESH,
        )

    def scatter(src, dst, i):
        made = [pltpu.make_async_copy(src(chip), dst, recv.at[i])]
        for to, device in peers:
            made.append(
                pltpu.make_async_remote_copy(
                    src_ref=src(to), dst_ref=dst, send_sem=send.at[i], recv_sem=recv.at[i],
                    device_id=device, device_id_type=MESH,
                )
            )
        return made[1:] + made[:1]

    def arrived(whole, i):
        pltpu.make_async_copy(whole, whole, recv.at[i]).wait()

    firsts = [pair(sa.at[q], sb.at[q, core], q) for q in range(PARTS)]
    for copy in firsts:
        copy.start()
    sb6 = sb.reshape(PARTS, 2, CHIPS, 1, N)
    rf6 = rf.reshape(PARTS, CHIPS, 2, 1, N)
    sr6 = sr.reshape(PARTS, CHIPS, 2, 1, N)
    rb6 = rb.reshape(PARTS, 2, CHIPS, 1, N)
    for q in range(PARTS):
        firsts[q].wait_recv()
        for copy in scatter(lambda to: sb6.at[q, :, to], rf6.at[q, chip], PARTS + q):
            copy.start()

    waiting = []

    def emit(count):
        for _ in range(min(count, len(waiting))):
            waiting.pop(0).start()

    for q in range(PARTS):
        emit(FIRST)
        arrived(rf.at[q], PARTS + q)
        blocks = swap([rf[q, pl.ds(8 * i, 8), :] for i in range(16)])
        emit(16)
        high, low = split(jnp.concatenate(blocks, 0))
        wide = dot(jnp.concatenate([high, low], 1), y_ref[: 2 * N, :]) + dot(high, y_ref[2 * N :, :])
        emit(16)
        high, low = split(wide)
        both = jnp.concatenate([high, low], 0)
        plane = kernel_ref[...]
        wide_plane = jnp.concatenate([plane, plane], 1)
        halves = []
        for half in range(2):
            rows = slice(half * N, (half + 1) * N)
            freq = dot(x_ref[rows, : 2 * N], both) + dot(x_ref[rows, 2 * N :], high)
            halves.append(split(freq * wide_plane))
            emit(16)
        high = jnp.concatenate([halves[0][0], halves[1][0]], 0)
        low = jnp.concatenate([halves[0][1], halves[1][1]], 0)
        mixed = dot(xb_ref[:N, :], high) + dot(xb_ref[:N, :], low) + dot(xb_ref[N:, :], high)
        emit(CHIPS)
        high, low = split(mixed)
        twice = dot(high, yb_ref[...])
        cells = twice[:, :N] + twice[:, N:] + dot(low, yb_ref[:, :N])
        blocks = swap([cells[8 * i : 8 * i + 8] for i in range(16)])
        for i in range(16):
            sr[q, pl.ds(8 * i, 8), :] = blocks[i]
        waiting += scatter(lambda to, q=q: sr6.at[q, to], rb6.at[q, :, chip], 2 * PARTS + q)
    emit(CHIPS)

    lasts = [pair(rb.at[q, other], pb.at[q], 3 * PARTS + q) for q in range(PARTS)]
    for q in range(PARTS):
        arrived(rb.at[q], 2 * PARTS + q)
        lasts[q].start()
        if q % 2 == 0:
            continue
        r = q // 2
        field = jnp.zeros((N, N), F32)
        for owner, mine in ((core, True), (other, False)):
            if not mine:
                lasts[q - 1].wait_recv()
                lasts[q].wait_recv()
            pieces_of = [rb[i, core] if mine else pb[i] for i in (q - 1, q)]
            high, low = split(jnp.concatenate(pieces_of, 0))
            twice = dot(high, zb_ref[owner], ((0,), (0,)))
            field += twice[:, :N] + twice[:, N:] + dot(low, zb_ref[owner, :, :N], ((0,), (0,)))
        out[r] = field.reshape(16, 8, N)
    for copy in firsts + lasts:
        copy.wait_send()
    for i in range(PARTS, 3 * PARTS):
        some = rf6.at[0, pl.ds(0, CHIPS - 1)]
        pltpu.make_async_copy(some, some, send.at[i]).wait()


def body(density, kernel_factors):
    made = tables()
    held = [pltpu.VMEM(density.shape, F32), pltpu.VMEM(kernel_factors.shape[:2] + (N,), F32)]
    held += [pltpu.VMEM(table.shape, BF16) for table in made]
    scratch = [
        pltpu.VMEM((PARTS, CHIPS, N), F32),
        pltpu.VMEM((PARTS, 2, CHIPS, N), F32),
        pltpu.VMEM((PARTS, N, N), F32),
        pltpu.VMEM((PARTS, N, N), F32),
        pltpu.VMEM((PARTS, 2, CHIPS, N), F32),
        pltpu.VMEM((PARTS, CHIPS, N), F32),
        pltpu.VMEM((N, N), F32),
        pltpu.SemaphoreType.DMA((8,)),
        pltpu.SemaphoreType.DMA((4 * PARTS,)),
        pltpu.SemaphoreType.DMA((4 * PARTS,)),
    ]
    return pl.pallas_call(
        kernel,
        out_shape=jax.ShapeDtypeStruct(density.shape, F32),
        in_specs=[pl.BlockSpec(memory_space=pl.ANY)] * (2 + len(made)),
        out_specs=pl.BlockSpec(memory_space=pltpu.VMEM),
        scratch_shapes=held + scratch,
        compiler_params=pltpu.CompilerParams(collective_id=0, has_side_effects=True),
        name="solve",
    )(density, kernel_factors, *[jnp.asarray(table) for table in made])


def solution(mesh):
    return jax.shard_map(
        body,
        mesh=mesh,
        in_specs=(P("rep", "px", "py", None), P()),
        out_specs=P("rep", "px", "py", None),
        check_vma=False,
    )
```

time: 38.1 us -> 34 us (0.89)
  Pallas kernels: 36.4 us -> 32.3 us
    pallas_call x1, Pallas kernels: 36.4 us -> 32.3 us  [body(): pl.pallas_call(kernel, out_shape=jax.ShapeDtypeStruct(density.shape, F32)...]
where the time goes in v2:
time: 34 us; the launch traced here: 33.9 us
  Pallas kernels  32.3 us (95%)
  local copies, waits for them, and re-layouts  1.57 us (5%)
    pallas_call x1, Pallas kernels, body(): pl.pallas_call(kernel, out_shape=jax.ShapeDtypeStruct(density.shape, F32)...  32.3 us
    unnamed x1, local copies, waits for them, and re-layouts  1.57 us

profile of v2, /device:TPU:1, one launch (start us, length us, event | category | flops | bytes accessed | tf_op | source)
XLA Modules:
  0.0 33.9 jit_solution(12997047237230035876)
XLA Ops:
  0.0 32.3 %solve.1 = f32[2,16,8,128]{3,2,1,0:T(8,128)} custom-call(f32[2,16,8,128]{3,2,1,0:T(8,128)} %density.1, f32[3,89,256]{2,1,0:T(8,128)} %factors.1, bf16[2,128,384]{2,1,0:T(8,128)(2,1)} %constant.12.clone.t_z, bf16[384,256]{1,0:T(8,128)(2,1)} %constant.13.clone.t_y, bf16[256,384]{1,0:T(8,128)(2,1)} %constant.14.clone.t_x, ...), custom_call_target="tpu_custom_call" | custom-call | tf_op jit(solution)/shard_map/solve/pallas_call | solution.py:259
  32.3 1.6 %copy.10 = f32[2,16,8,128]{3,2,1,0:T(8,128)} copy(f32[2,16,8,128]{3,2,1,0:T(8,128)} %solve.1) | data formatting | bytes 262144

commit v3 on v2

--- a/solution.py
+++ b/solution.py
@@ -14,7 +14,10 @@
 ROWS_Y = 4
 F32, BF16 = jnp.float32, jnp.bfloat16
 PARTS = 4
-FIRST = 0
+OUT = ((0, 1), (1, 1), (2, 1), (3, 1))
+BACK = ((0, 1), (1, 1), (2, 1), (3, 1))
+DIRECT = (3,)
+PIECE = (0, 16, 16, 16, 16, 128)
 
 
 def order():
@@ -39,7 +42,7 @@
     cos, sin = np.cos(angle), np.sin(angle)
     weight = np.where(k == 0, 1.0, 2.0)[:, None] / (2 * N)
     by_owner = np.stack([cos, sin], 0).reshape(2, 2, CHIPS, N).swapaxes(0, 1).reshape(2, 2 * CHIPS, N)
-    by_owner_back = np.stack([cos * weight, sin * weight], 0).reshape(2, 2, CHIPS, N).swapaxes(0, 1).reshape(2, 2 * CHIPS, N)
+    by_owner_back = np.stack([cos * weight, sin * weight], 0).reshape(2, 2, CHIPS, N)
     plain = np.concatenate([cos, sin], 0)
     back = np.concatenate([cos * weight, sin * weight], 0)
     cells = np.arange(N).reshape(8, 16).T.reshape(-1)
@@ -55,7 +58,7 @@
     high, low = pieces(back)
     out.append(np.concatenate([high, low], 1))
     high, low = pieces(by_owner_back)
-    out.append(np.concatenate([high, low], 2))
+    out.append(np.concatenate([high, low], 3))
     return out
 
 
@@ -154,7 +157,7 @@
         )
 
     def scatter(src, dst, i):
-        made = [pltpu.make_async_copy(src(chip), dst, recv.at[i])]
+        made = []
         for to, device in peers:
             made.append(
                 pltpu.make_async_remote_copy(
@@ -162,37 +165,45 @@
                     device_id=device, device_id_type=MESH,
                 )
             )
-        return made[1:] + made[:1]
+        return made + [pltpu.make_async_copy(src(chip), dst, recv.at[i])]
 
     def arrived(whole, i):
         pltpu.make_async_copy(whole, whole, recv.at[i]).wait()
 
-    firsts = [pair(sa.at[q], sb.at[q, core], q) for q in range(PARTS)]
-    for copy in firsts:
-        copy.start()
     sb6 = sb.reshape(PARTS, 2, CHIPS, 1, N)
     rf6 = rf.reshape(PARTS, CHIPS, 2, 1, N)
     sr6 = sr.reshape(PARTS, CHIPS, 2, 1, N)
     rb6 = rb.reshape(PARTS, 2, CHIPS, 1, N)
+    sent = []
+
+    def drain(whole, i):
+        sent.append((whole, i))
+
+    firsts = [pair(sa.at[pl.ds(q, n)], sb.at[pl.ds(q, n), core], q) for q, n in OUT]
+    for copy in firsts:
+        copy.start()
+    for i, (q, n) in enumerate(OUT):
+        firsts[i].wait_recv()
+        for copy in scatter(lambda to: sb6.at[pl.ds(q, n), :, to], rf6.at[pl.ds(q, n), chip], PARTS + q):
+            copy.start()
+        drain(rf6.at[pl.ds(q, n), pl.ds(0, CHIPS - 1)], PARTS + q)
+
+    waiting = []
+
+    def emit(point):
+        for _ in range(min(PIECE[point], len(waiting))):
+            waiting.pop(0).start()
+
     for q in range(PARTS):
-        firsts[q].wait_recv()
-        for copy in scatter(lambda to: sb6.at[q, :, to], rf6.at[q, chip], PARTS + q):
-            copy.start()
-
-    waiting = []
-
-    def emit(count):
-        for _ in range(min(count, len(waiting))):
-            waiting.pop(0).start()
-
-    for q in range(PARTS):
-        emit(FIRST)
-        arrived(rf.at[q], PARTS + q)
+        emit(0)
+        for start, n in OUT:
+            if start == q:
+                arrived(rf.at[pl.ds(q, n)], PARTS + q)
         blocks = swap([rf[q, pl.ds(8 * i, 8), :] for i in range(16)])
-        emit(16)
+        emit(1)
         high, low = split(jnp.concatenate(blocks, 0))
         wide = dot(jnp.concatenate([high, low], 1), y_ref[: 2 * N, :]) + dot(high, y_ref[2 * N :, :])
-        emit(16)
+        emit(2)
         high, low = split(wide)
         both = jnp.concatenate([high, low], 0)
         plane = kernel_ref[...]
@@ -202,42 +213,72 @@
             rows = slice(half * N, (half + 1) * N)
             freq = dot(x_ref[rows, : 2 * N], both) + dot(x_ref[rows, 2 * N :], high)
             halves.append(split(freq * wide_plane))
-            emit(16)
+            emit(3 + half)
         high = jnp.concatenate([halves[0][0], halves[1][0]], 0)
         low = jnp.concatenate([halves[0][1], halves[1][1]], 0)
         mixed = dot(xb_ref[:N, :], high) + dot(xb_ref[:N, :], low) + dot(xb_ref[N:, :], high)
-        emit(CHIPS)
+        emit(5)
         high, low = split(mixed)
         twice = dot(high, yb_ref[...])
         cells = twice[:, :N] + twice[:, N:] + dot(low, yb_ref[:, :N])
         blocks = swap([cells[8 * i : 8 * i + 8] for i in range(16)])
         for i in range(16):
             sr[q, pl.ds(8 * i, 8), :] = blocks[i]
-        waiting += scatter(lambda to, q=q: sr6.at[q, to], rb6.at[q, :, chip], 2 * PARTS + q)
-    emit(CHIPS)
-
-    lasts = [pair(rb.at[q, other], pb.at[q], 3 * PARTS + q) for q in range(PARTS)]
+        if q in DIRECT:
+            flag = 2 * PARTS + q
+            for to, device in peers:
+                for core_to in (core, other):
+                    waiting.append(
+                        pltpu.make_async_remote_copy(
+                            src_ref=sr6.at[q, to, core_to], dst_ref=rb6.at[q, core, chip],
+                            send_sem=send.at[flag], recv_sem=recv.at[flag],
+                            device_id={"px": device["px"] + core_to - core, "py": device["py"]}, device_id_type=MESH,
+                        )
+                    )
+            waiting.append(pair(sr6.at[q, chip, other], rb6.at[q, core, chip], flag))
+            waiting.append(pltpu.make_async_copy(sr6.at[q, chip, core], rb6.at[q, core, chip], recv.at[flag]))
+            drain(rf.reshape(PARTS, N, 1, N).at[q, pl.ds(0, N - 1)], flag)
+        else:
+            for start, n in BACK:
+                if start + n - 1 == q:
+                    some = pl.ds(start, n)
+                    waiting += scatter(lambda to, some=some: sr6.at[some, to], rb6.at[some, :, chip], 2 * PARTS + start)
+                    drain(rf6.at[some, pl.ds(0, CHIPS - 1)], 2 * PARTS + start)
+    for copy in waiting:
+        copy.start()
+
+    def back(rows, table):
+        high, low = split(rows)
+        twice = dot(high, table, ((0,), (0,)))
+        return twice[:, :N] + twice[:, N:] + dot(low, table[:, :N], ((0,), (0,)))
+
+    lasts, fields = {}, [None, None]
+
+    def add(r, part):
+        fields[r] = part if fields[r] is None else fields[r] + part
+
+    groups = [g for g in BACK if g[0] not in DIRECT]
+    for start, n in groups:
+        arrived(rb.at[pl.ds(start, n)], 2 * PARTS + start)
+        lasts[start] = pair(rb.at[pl.ds(start, n), other], pb.at[pl.ds(start, n)], 3 * PARTS + start)
+        lasts[start].start()
+    for start, n in groups:
+        for q in range(start, start + n):
+            add(q // 2, back(rb[q, core], zb_ref[q % 2, core]))
+    for start, n in groups:
+        lasts[start].wait_recv()
+        for q in range(start, start + n):
+            add(q // 2, back(pb[q], zb_ref[q % 2, other]))
     for q in range(PARTS):
-        arrived(rb.at[q], 2 * PARTS + q)
-        lasts[q].start()
-        if q % 2 == 0:
-            continue
-        r = q // 2
-        field = jnp.zeros((N, N), F32)
-        for owner, mine in ((core, True), (other, False)):
-            if not mine:
-                lasts[q - 1].wait_recv()
-                lasts[q].wait_recv()
-            pieces_of = [rb[i, core] if mine else pb[i] for i in (q - 1, q)]
-            high, low = split(jnp.concatenate(pieces_of, 0))
-            twice = dot(high, zb_ref[owner], ((0,), (0,)))
-            field += twice[:, :N] + twice[:, N:] + dot(low, zb_ref[owner, :, :N], ((0,), (0,)))
-        out[r] = field.reshape(16, 8, N)
-    for copy in firsts + lasts:
+        if q in DIRECT:
+            arrived(rb.at[q], 2 * PARTS + q)
+            add(q // 2, back(rb[q].reshape(N, N), zb_ref[q % 2].reshape(N, 2 * N)))
+    for r in range(2):
+        out[r] = fields[r].reshape(16, 8, N)
+    for copy in firsts + list(lasts.values()):
         copy.wait_send()
-    for i in range(PARTS, 3 * PARTS):
-        some = rf6.at[0, pl.ds(0, CHIPS - 1)]
-        pltpu.make_async_copy(some, some, send.at[i]).wait()
+    for whole, i in sent:
+        pltpu.make_async_copy(whole, whole, send.at[i]).wait()
 
 
 def body(density, kernel_factors):
@@ -258,7 +299,7 @@
     ]
     return pl.pallas_call(
         kernel,
-        out_shape=jax.ShapeDtypeStruct(density.shape, F32),
+        out_shape=pltpu.VMEM(density.shape, F32),
         in_specs=[pl.BlockSpec(memory_space=pl.ANY)] * (2 + len(made)),
         out_specs=pl.BlockSpec(memory_space=pltpu.VMEM),
         scratch_shapes=held + scratch,

time: 34 us -> 31.3 us (0.921)
  Pallas kernels: 32.3 us -> 30.6 us
  local copies, waits for them, and re-layouts: 1.57 us -> 0.66 us
    pallas_call x1, Pallas kernels: 32.3 us -> 30.6 us  [body(): pl.pallas_call(kernel, out_shape=pltpu.VMEM(density.shape, F32), in_specs...]
    unnamed x1, local copies, waits for them, and re-layouts: 1.57 us -> 0.66 us
where the time goes in v3:
time: 31.3 us; the launch traced here: 31.2 us
  Pallas kernels  30.6 us (98%)
  local copies, waits for them, and re-layouts  0.66 us (2%)
    pallas_call x1, Pallas kernels, body(): pl.pallas_call(kernel, out_shape=pltpu.VMEM(density.shape, F32), in_specs...  30.6 us
    unnamed x1, local copies, waits for them, and re-layouts  0.66 us

profile of v3, /device:TPU:1, one launch (start us, length us, event | category | flops | bytes accessed | tf_op | source)
XLA Modules:
  0.0 31.2 jit_solution(1646213652103431099)
XLA Ops:
  0.0 30.6 %solve.1 = f32[2,16,8,128]{3,2,1,0:T(8,128)S(1)} custom-call(f32[2,16,8,128]{3,2,1,0:T(8,128)} %density.1, f32[3,89,256]{2,1,0:T(8,128)} %factors.1, bf16[2,128,384]{2,1,0:T(8,128)(2,1)} %constant.12.clone.t_z, bf16[384,256]{1,0:T(8,128)(2,1)} %constant.13.clone.t_y, bf16[256,384]{1,0:T(8,128)(2,1)} %constant.14.clone.t_x, ...), custom_call_target="tpu_custom_call" | custom-call | tf_op jit(solution)/shard_map/solve/pallas_call | solution.py:300
  30.6 0.7 %copy.10 = f32[2,16,8,128]{3,2,1,0:T(8,128)} copy(f32[2,16,8,128]{3,2,1,0:T(8,128)S(1)} %solve.1) | data formatting | bytes 262144

commit v4 on v2

--- a/solution.py
+++ b/solution.py
@@ -14,13 +14,17 @@
 ROWS_Y = 4
 F32, BF16 = jnp.float32, jnp.bfloat16
 PARTS = 4
-FIRST = 0
+PIECE = (0, 24, 24, 24, 24, 24)
 
 
 def order():
     steps = [(y, z, x) for y in (0, 1, 3, 2) for x in (0, 1) for z in (0, 1, 7, 2, 6, 3, 5, 4) if y or x or z]
     steps = [steps[i] for i in np.random.RandomState(0).permutation(len(steps))]
-    return sorted(steps, key=lambda s: -(min(s[0], 4 - s[0]) + min(s[1], 8 - s[1]) + s[2]))
+    return sorted(steps, key=lambda s: -hops(s))
+
+
+def hops(s):
+    return min(s[0], 4 - s[0]) + min(s[1], 8 - s[1]) + s[2]
 
 
 ORDER = order()
@@ -39,7 +43,7 @@
     cos, sin = np.cos(angle), np.sin(angle)
     weight = np.where(k == 0, 1.0, 2.0)[:, None] / (2 * N)
     by_owner = np.stack([cos, sin], 0).reshape(2, 2, CHIPS, N).swapaxes(0, 1).reshape(2, 2 * CHIPS, N)
-    by_owner_back = np.stack([cos * weight, sin * weight], 0).reshape(2, 2, CHIPS, N).swapaxes(0, 1).reshape(2, 2 * CHIPS, N)
+    by_owner_back = np.stack([cos * weight, sin * weight], 0).reshape(2, 2, CHIPS, N)
     plain = np.concatenate([cos, sin], 0)
     back = np.concatenate([cos * weight, sin * weight], 0)
     cells = np.arange(N).reshape(8, 16).T.reshape(-1)
@@ -55,7 +59,7 @@
     high, low = pieces(back)
     out.append(np.concatenate([high, low], 1))
     high, low = pieces(by_owner_back)
-    out.append(np.concatenate([high, low], 2))
+    out.append(np.concatenate([high, low], 3))
     return out
 
 
@@ -87,27 +91,26 @@
 def kernel(
     density, factors, t_z, t_y, t_x, t_xb, t_yb, t_zb, out,
     d_ref, f_ref, z_ref, y_ref, x_ref, xb_ref, yb_ref, zb_ref,
-    sa, sb, rf, sr, rb, pb, kernel_ref,
-    load, send, recv,
+    sa, sb, rf, sr, rb, kernel_ref,
+    load, send, recv, ready,
 ):
     px, py = lax.axis_index("px"), lax.axis_index("py")
     core, y_chip = lax.rem(px, 2), lax.div(px, 2)
     x_chip, z_chip = lax.rem(py, 2), lax.div(py, 2)
     other = 1 - core
     chip = py * ROWS_Y + y_chip
-    partner = {"px": px + 1 - 2 * core}
     ys = [lax.rem(y_chip + i, 4) for i in range(4)]
     zs = [lax.rem(z_chip + i, 8) for i in range(8)]
     xs = [x_chip, 1 - x_chip]
     peers = []
     for y, z, x in ORDER:
         to = zs[z] * 2 + xs[x]
-        peers.append((to * ROWS_Y + ys[y], {"px": ys[y] * 2 + core, "py": to}))
+        peers.append((hops((y, z, x)), to * ROWS_Y + ys[y], ys[y] * 2, to))
 
     barrier = pltpu.get_barrier_semaphore()
-    for _, device in peers:
-        pl.semaphore_signal(barrier, inc=1, device_id=device, device_id_type=MESH)
-    pl.semaphore_signal(barrier, inc=1, device_id=partner, device_id_type=MESH)
+    for _, _, to_px, to_py in peers:
+        pl.semaphore_signal(barrier, inc=1, device_id={"px": to_px + core, "py": to_py}, device_id_type=MESH)
+    pl.semaphore_signal(barrier, inc=1, device_id={"px": 2 * y_chip + other, "py": py}, device_id_type=MESH)
 
     loads = [
         pltpu.make_async_copy(src, dst, load.at[i])
@@ -147,52 +150,53 @@
 
     pl.semaphore_wait(barrier, CHIPS)
 
-    def pair(src, dst, i):
+    def push(src, dst, i, to_px, to_py):
         return pltpu.make_async_remote_copy(
             src_ref=src, dst_ref=dst, send_sem=send.at[i], recv_sem=recv.at[i],
-            device_id=partner, device_id_type=MESH,
+            device_id={"px": to_px, "py": to_py}, device_id_type=MESH,
         )
-
-    def scatter(src, dst, i):
-        made = [pltpu.make_async_copy(src(chip), dst, recv.at[i])]
-        for to, device in peers:
-            made.append(
-                pltpu.make_async_remote_copy(
-                    src_ref=src(to), dst_ref=dst, send_sem=send.at[i], recv_sem=recv.at[i],
-                    device_id=device, device_id_type=MESH,
-                )
-            )
-        return made[1:] + made[:1]
 
     def arrived(whole, i):
         pltpu.make_async_copy(whole, whole, recv.at[i]).wait()
 
-    firsts = [pair(sa.at[q], sb.at[q, core], q) for q in range(PARTS)]
-    for copy in firsts:
-        copy.start()
     sb6 = sb.reshape(PARTS, 2, CHIPS, 1, N)
     rf6 = rf.reshape(PARTS, CHIPS, 2, 1, N)
     sr6 = sr.reshape(PARTS, CHIPS, 2, 1, N)
     rb6 = rb.reshape(PARTS, 2, CHIPS, 1, N)
+    rows_of = rf.reshape(PARTS, N, 1, N)
+
+    pl.semaphore_signal(ready, inc=1, device_id={"px": 2 * y_chip + other, "py": py}, device_id_type=MESH)
+    between = push(sa.at[pl.ds(1, PARTS - 1)], sb.at[pl.ds(1, PARTS - 1), core], 0, 2 * y_chip + other, py)
+    between.start()
+    sa6 = sa.reshape(PARTS, CHIPS, 1, N)
+    first = rf6.at[0, chip, core]
+    for _, to, to_px, to_py in peers:
+        push(sb6.at[0, core, to], first, 1, to_px + core, to_py).start()
+    pl.semaphore_wait(ready, 1)
+    for _, to, to_px, to_py in peers:
+        push(sa6.at[0, to], first, 1, to_px + other, to_py).start()
+    push(sa6.at[0, chip], first, 1, 2 * y_chip + other, py).start()
+    pltpu.make_async_copy(sb6.at[0, core, chip], first, recv.at[1]).start()
+    between.wait_recv()
+    for q in range(1, PARTS):
+        for _, to, to_px, to_py in peers:
+            push(sb6.at[q, :, to], rf6.at[q, chip], 1 + q, to_px + core, to_py).start()
+        pltpu.make_async_copy(sb6.at[q, :, chip], rf6.at[q, chip], recv.at[1 + q]).start()
+
+    waiting = []
+
+    def emit(point):
+        for _ in range(min(PIECE[point], len(waiting))):
+            waiting.pop(0)[1].start()
+
     for q in range(PARTS):
-        firsts[q].wait_recv()
-        for copy in scatter(lambda to: sb6.at[q, :, to], rf6.at[q, chip], PARTS + q):
-            copy.start()
-
-    waiting = []
-
-    def emit(count):
-        for _ in range(min(count, len(waiting))):
-            waiting.pop(0).start()
-
-    for q in range(PARTS):
-        emit(FIRST)
-        arrived(rf.at[q], PARTS + q)
+        emit(0)
+        arrived(rf.at[q], 1 + q)
         blocks = swap([rf[q, pl.ds(8 * i, 8), :] for i in range(16)])
-        emit(16)
+        emit(1)
         high, low = split(jnp.concatenate(blocks, 0))
         wide = dot(jnp.concatenate([high, low], 1), y_ref[: 2 * N, :]) + dot(high, y_ref[2 * N :, :])
-        emit(16)
+        emit(2)
         high, low = split(wide)
         both = jnp.concatenate([high, low], 0)
         plane = kernel_ref[...]
@@ -202,42 +206,44 @@
             rows = slice(half * N, (half + 1) * N)
             freq = dot(x_ref[rows, : 2 * N], both) + dot(x_ref[rows, 2 * N :], high)
             halves.append(split(freq * wide_plane))
-            emit(16)
+            emit(3 + half)
         high = jnp.concatenate([halves[0][0], halves[1][0]], 0)
         low = jnp.concatenate([halves[0][1], halves[1][1]], 0)
         mixed = dot(xb_ref[:N, :], high) + dot(xb_ref[:N, :], low) + dot(xb_ref[N:, :], high)
-        emit(CHIPS)
+        emit(5)
         high, low = split(mixed)
         twice = dot(high, yb_ref[...])
         cells = twice[:, :N] + twice[:, N:] + dot(low, yb_ref[:, :N])
         blocks = swap([cells[8 * i : 8 * i + 8] for i in range(16)])
         for i in range(16):
             sr[q, pl.ds(8 * i, 8), :] = blocks[i]
-        waiting += scatter(lambda to, q=q: sr6.at[q, to], rb6.at[q, :, chip], 2 * PARTS + q)
-    emit(CHIPS)
-
-    lasts = [pair(rb.at[q, other], pb.at[q], 3 * PARTS + q) for q in range(PARTS)]
+        flag = 1 + PARTS + q
+        for far, to, to_px, to_py in peers:
+            for core_to in (core, other):
+                waiting.append((far, push(sr6.at[q, to, core_to], rb6.at[q, core, chip], flag, to_px + core_to, to_py)))
+        waiting.append((0, push(sr6.at[q, chip, other], rb6.at[q, core, chip], flag, 2 * y_chip + other, py)))
+        waiting.append((0, pltpu.make_async_copy(sr6.at[q, chip, core], rb6.at[q, core, chip], recv.at[flag])))
+        waiting.sort(key=lambda pair: -pair[0])
+    for _, copy in waiting:
+        copy.start()
+
+    def back(rows, table):
+        high, low = split(rows)
+        twice = dot(high, table, ((0,), (0,)))
+        return twice[:, :N] + twice[:, N:] + dot(low, table[:, :N], ((0,), (0,)))
+
+    for r in range(2):
+        field = None
+        for q in (2 * r, 2 * r + 1):
+            arrived(rb.at[q], 1 + PARTS + q)
+            part = back(rb[q].reshape(N, N), zb_ref[q % 2].reshape(N, 2 * N))
+            field = part if field is None else field + part
+        out[r] = field.reshape(16, 8, N)
+    between.wait_send()
     for q in range(PARTS):
-        arrived(rb.at[q], 2 * PARTS + q)
-        lasts[q].start()
-        if q % 2 == 0:
-            continue
-        r = q // 2
-        field = jnp.zeros((N, N), F32)
-        for owner, mine in ((core, True), (other, False)):
-            if not mine:
-                lasts[q - 1].wait_recv()
-                lasts[q].wait_recv()
-            pieces_of = [rb[i, core] if mine else pb[i] for i in (q - 1, q)]
-            high, low = split(jnp.concatenate(pieces_of, 0))
-            twice = dot(high, zb_ref[owner], ((0,), (0,)))
-            field += twice[:, :N] + twice[:, N:] + dot(low, zb_ref[owner, :, :N], ((0,), (0,)))
-        out[r] = field.reshape(16, 8, N)
-    for copy in firsts + lasts:
-        copy.wait_send()
-    for i in range(PARTS, 3 * PARTS):
-        some = rf6.at[0, pl.ds(0, CHIPS - 1)]
-        pltpu.make_async_copy(some, some, send.at[i]).wait()
+        out_of = rows_of.at[q, pl.ds(0, N - 1)] if q == 0 else rf6.at[q, pl.ds(0, CHIPS - 1)]
+        for some, i in ((out_of, 1 + q), (rows_of.at[q, pl.ds(0, N - 1)], 1 + PARTS + q)):
+            pltpu.make_async_copy(some, some, send.at[i]).wait()
 
 
 def body(density, kernel_factors):
@@ -250,15 +256,15 @@
         pltpu.VMEM((PARTS, N, N), F32),
         pltpu.VMEM((PARTS, N, N), F32),
         pltpu.VMEM((PARTS, 2, CHIPS, N), F32),
-        pltpu.VMEM((PARTS, CHIPS, N), F32),
         pltpu.VMEM((N, N), F32),
         pltpu.SemaphoreType.DMA((8,)),
-        pltpu.SemaphoreType.DMA((4 * PARTS,)),
-        pltpu.SemaphoreType.DMA((4 * PARTS,)),
+        pltpu.SemaphoreType.DMA((1 + 2 * PARTS,)),
+        pltpu.SemaphoreType.DMA((1 + 2 * PARTS,)),
+        pltpu.SemaphoreType.REGULAR,
     ]
     return pl.pallas_call(
         kernel,
-        out_shape=jax.ShapeDtypeStruct(density.shape, F32),
+        out_shape=pltpu.VMEM(density.shape, F32),
         in_specs=[pl.BlockSpec(memory_space=pl.ANY)] * (2 + len(made)),
         out_specs=pl.BlockSpec(memory_space=pltpu.VMEM),
         scratch_shapes=held + scratch,

time: 34 us -> 30.9 us (0.909)
  Pallas kernels: 32.3 us -> 30.1 us
  local copies, waits for them, and re-layouts: 1.57 us -> 0.66 us
    pallas_call x1, Pallas kernels: 32.3 us -> 30.1 us  [body(): pl.pallas_call(kernel, out_shape=pltpu.VMEM(density.shape, F32), in_specs...]
    unnamed x1, local copies, waits for them, and re-layouts: 1.57 us -> 0.66 us
where the time goes in v4:
time: 30.9 us; the launch traced here: 30.8 us
  Pallas kernels  30.1 us (97%)
  local copies, waits for them, and re-layouts  0.66 us (2%)
    pallas_call x1, Pallas kernels, body(): pl.pallas_call(kernel, out_shape=pltpu.VMEM(density.shape, F32), in_specs...  30.1 us
    unnamed x1, local copies, waits for them, and re-layouts  0.66 us

profile of v4, /device:TPU:1, one launch (start us, length us, event | category | flops | bytes accessed | tf_op | source)
XLA Modules:
  0.0 30.8 jit_solution(5352048500365789837)
XLA Ops:
  0.0 30.1 %solve.1 = f32[2,16,8,128]{3,2,1,0:T(8,128)S(1)} custom-call(f32[2,16,8,128]{3,2,1,0:T(8,128)} %density.1, f32[3,89,256]{2,1,0:T(8,128)} %factors.1, bf16[2,128,384]{2,1,0:T(8,128)(2,1)} %constant.12.clone.t_z, bf16[384,256]{1,0:T(8,128)(2,1)} %constant.13.clone.t_y, bf16[256,384]{1,0:T(8,128)(2,1)} %constant.14.clone.t_x, ...), custom_call_target="tpu_custom_call" | custom-call | tf_op jit(solution)/shard_map/solve/pallas_call | solution.py:265
  30.1 0.7 %copy.10 = f32[2,16,8,128]{3,2,1,0:T(8,128)} copy(f32[2,16,8,128]{3,2,1,0:T(8,128)S(1)} %solve.1) | data formatting | bytes 262144
